TPU v7x, 32 devices: a 4x2x2 block of a 4x4x8 slice. The times are simulated.
32 devices in a mesh: dp: 4 (over y, z), dcp: 8 (over x, core).
Axes of the slice: x: 4, y: 2, z: 2, core: 2. Of those that a mesh axis runs over, the one named last changes fastest.
The devices are a block of a 4x4x8 slice.
Arguments:
- q_abs: bfloat16 [128, 2, 64, 576], P('dp', None, 'dcp'), parts along dimension 0
- kv_cache: bfloat16 [128, 16, 8, 64, 576], P('dp', None, 'dcp'), parts along dimension 0
- lengths: int32 [128], P('dp'), parts along dimension 0
Outputs:
- output: bfloat16 [128, 2, 64, 512], P('dp', None, 'dcp'), parts along dimension 0
There are 4 independent parts. A program takes and returns all parts, laid end to end along the dimension named above; each array names one.
All inputs are finite; a program needn't handle non-finite values.
Results may differ from a plain program's by a relative error of at most 0.00757035.
Values are sent between devices in bfloat16 or wider.
A program may use at most 768 MiB of HBM per device.

v0:
```python
import jax
import jax.numpy as jnp
from jax import lax
from jax.sharding import PartitionSpec as P

LATENT = 512
ROPE = 64
NOPE = 128
PAGE = 64
MASKED = -1e30


def solution(mesh):
    group_size = mesh.shape['dcp']
    score_scale = (NOPE + ROPE) ** -0.5

    def local_step(q_blk, kv_blk, len_blk):
        batch_loc, tok_count, heads_loc, q_width = q_blk.shape
        rounds = kv_blk.shape[1]
        local_keys = kv_blk.reshape(batch_loc, rounds * PAGE, q_width)
        q_all = lax.all_gather(q_blk, 'dcp', axis=2, tiled=True)
        scores = jnp.einsum('bthd,bsd->bths', q_all, local_keys, preferred_element_type=jnp.float32) * score_scale
        device = lax.axis_index('dcp')
        positions = ((jnp.arange(rounds)[:, None] * group_size + device) * PAGE + jnp.arange(PAGE)[None, :]).reshape(rounds * PAGE)
        last_pos = len_blk[:, None] - tok_count + jnp.arange(tok_count)[None, :]
        visible = positions[None, None, None, :] <= last_pos[:, :, None, None]
        scores = jnp.where(visible, scores, MASKED)
        row_max = jnp.max(scores, axis=-1)
        weights = jnp.exp(scores - row_max[..., None])
        row_sum = jnp.sum(weights, axis=-1)
        part_out = jnp.einsum('bths,bsc->bthc', weights.astype(jnp.bfloat16), local_keys[:, :, :LATENT], preferred_element_type=jnp.float32)
        part_out = (part_out / row_sum[..., None]).astype(jnp.bfloat16)
        part_lse = row_max + jnp.log(row_sum)
        recv_out = lax.all_to_all(part_out, 'dcp', 2, 2, tiled=True).reshape(batch_loc, tok_count, group_size, heads_loc, LATENT)
        recv_lse = lax.all_to_all(part_lse, 'dcp', 2, 2, tiled=True).reshape(batch_loc, tok_count, group_size, heads_loc)
        total_lse = jax.nn.logsumexp(recv_lse, axis=2, keepdims=True)
        merge_w = jnp.exp(recv_lse - total_lse)
        merged = jnp.sum(merge_w[..., None] * recv_out.astype(jnp.float32), axis=2)
        return merged.astype(jnp.bfloat16)

    return jax.shard_map(local_step, mesh=mesh, in_specs=(P('dp', None, 'dcp', None), P('dp', None, 'dcp', None, None), P('dp')), out_specs=P('dp', None, 'dcp', None), check_vma=False)
```

profile of v0, /device:TPU:81, one launch (start us, length us, event | category | flops | bytes accessed | tf_op | source)
XLA Modules:
  0.0 181.4 jit_solution(11156096812458074960)
XLA Ops:
  6.5 0.0 all-gather.2.cloned.1.call-start
  6.6 0.7 all-gather.2.cloned.1.call-update
  7.3 0.1 iota_add_fusion.1
  7.4 0.1 add.66
  7.5 0.7 broadcast_add_fusion
  8.1 0.1 iota_add_fusion
  8.2 0.2 broadcast_compare_fusion
  8.4 38.1 %all-gather.2.cloned.1.call-done = bf16[32,2,64,576]{3,2,1,0:T(8,128)(2,1)} async-done(((bf16[32,2,8,576]{3,2,1,0:T(8,128)(2,1)}), bf16[32,2,64,576]{3,2,1,0:T(8,128)(2,1)}) %all-gather.2.cloned.1.call-update) | async-done | bytes 4718608 | tf_op jit(solution)/shard_map/all_gather | solution.py:21
  46.5 25.4 %fusion.1 = (f32[32,2,64]{2,1,0:T(2,128)S(1)}, f32[32,2,64,1024]{3,2,1,0:T(8,128)}) fusion(pred[32,2,1024]{2,1,0:T(4,128)(4,1)S(1)} %broadcast_compare_fusion, bf16[32,2,64,576]{3,2,1,0:T(8,128)(2,1)} %all-gather.2.cloned.1.call-done, bf16[32,1024,576,1]{2,1,3,0:T(8,128)(2,1)} %bitcast.28), kind=kOutput, calls=%fused_computation.4 | convolution fusion | flops 4844417024 | bytes 59326464 | tf_op jit(solution)/shard_map/bthd,bsd->bths/dot_general | solution.py:22
  72.0 8.1 %fusion.3 = f32[32,2,64]{2,1,0:T(2,128)S(1)} fusion(f32[32,2,64,1024]{3,2,1,0:T(8,128)} %get-tuple-element.6, f32[32,2,64]{2,1,0:T(2,128)S(1)} %get-tuple-element.5, pred[32,2,1024]{2,1,0:T(4,128)(4,1)S(1)} %broadcast_compare_fusion), kind=kLoop, calls=%fused_computation.6 | loop fusion | flops 16773120 | bytes 16875520 | tf_op jit(solution)/shard_map/reduce_sum | solution.py:30
  80.1 0.1 copy.23
  80.1 0.7 reshape.89
  80.9 3.5 %all-to-all-start = ((f32[8,1,512]{2,1,0:T(1,128)}), f32[8,1,512]{2,1,0:T(1,128)S(1)}, u32[]{:S(2)}, u32[]{:S(2)}) async-start(f32[8,1,512]{2,1,0:T(1,128)} %reshape.89), calls=%async_computation | async-start | bytes 32768 | tf_op jit(solution)/shard_map/all_to_all | solution.py:35
  84.4 20.2 %divide_convert_fusion = bf16[32,2,64,512]{3,2,1,0:T(8,128)(2,1)} fusion(f32[32,2,64]{2,1,0:T(2,128)S(1)} %fusion.3, bf16[32,1024,576]{2,1,0:T(8,128)(2,1)} %bitcast.29, f32[32,2,64,1024]{3,2,1,0:T(8,128)} %get-tuple-element.6, f32[32,2,64]{2,1,0:T(2,128)S(1)} %get-tuple-element.5, pred[32,2,1024]{2,1,0:T(4,128)(4,1)S(1)} %broadcast_compare_fusion), kind=kOutput, calls=%fused_computation.9 | convolution fusion | flops 4315938816 | bytes 54624256 | tf_op jit(solution)/shard_map/bths,bsc->bthc/dot_general | solution.py:31
  104.6 8.4 %copy.26 = bf16[32,2,64,512]{3,1,0,2:T(2,128)(2,1)} copy(bf16[32,2,64,512]{3,2,1,0:T(8,128)(2,1)} %divide_convert_fusion) | data formatting | bytes 8388608 | tf_op jit(solution)/shard_map/convert_element_type | solution.py:32
  113.0 0.0 all-to-all-done
  113.0 5.0 %all-to-all-start.1 = ((bf16[32,2,64,512]{3,1,0,2:T(2,128)(2,1)}), bf16[32,2,64,512]{3,1,0,2:T(2,128)(2,1)}, u32[]{:S(2)}, u32[]{:S(2)}) async-start(bf16[32,2,64,512]{3,1,0,2:T(2,128)(2,1)} %copy.26), calls=%async_computation.1 | async-start | bytes 8388608 | tf_op jit(solution)/shard_map/all_to_all | solution.py:34
  118.0 0.5 broadcast.75
  118.5 0.7 reduce
  119.2 0.1 reshape.90
  119.4 0.5 copy.25
  119.9 46.8 %all-to-all-done.1 = bf16[32,2,64,512]{3,1,0,2:T(2,128)(2,1)} async-done(((bf16[32,2,64,512]{3,1,0,2:T(2,128)(2,1)}), bf16[32,2,64,512]{3,1,0,2:T(2,128)(2,1)}, u32[]{:S(2)}, u32[]{:S(2)}) %all-to-all-start.1) | async-done | bytes 4194336 | tf_op jit(solution)/shard_map/all_to_all | solution.py:34
  166.6 6.7 %fusion.5 = bf16[32,2,8,512]{3,1,0,2:T(2,128)(2,1)S(1)} fusion(bf16[32,2,8,8,512]{4,1,0,3,2:T(2,128)(2,1)} %bitcast.9, f32[32,2,8,8]{1,0,3,2:T(8,128)S(1)} %copy.25), kind=kLoop, calls=%fused_computation.8 | loop fusion | flops 6029312 | bytes 4734976 | tf_op jit(solution)/shard_map/reduce_sum | solution.py:38
  173.3 1.2 copy.27
  (7 shorter events, 0.1 us)
Async XLA Ops:
  6.5 40.0 %all-gather.2.cloned.1.call-start = ((), (), s32[]{:S(2)}) async-start(), calls=%async_computation.2 | async-start | bytes 5898240 | tf_op jit(solution)/shard_map/all_gather | solution.py:21
  80.9 32.1 %all-to-all-start = ((f32[8,1,512]{2,1,0:T(1,128)}), f32[8,1,512]{2,1,0:T(1,128)S(1)}, u32[]{:S(2)}, u32[]{:S(2)}) async-start(f32[8,1,512]{2,1,0:T(1,128)} %reshape.89), calls=%async_computation | async-start | bytes 32768 | tf_op jit(solution)/shard_map/all_to_all | solution.py:35
  113.0 53.6 %all-to-all-start.1 = ((bf16[32,2,64,512]{3,1,0,2:T(2,128)(2,1)}), bf16[32,2,64,512]{3,1,0,2:T(2,128)(2,1)}, u32[]{:S(2)}, u32[]{:S(2)}) async-start(bf16[32,2,64,512]{3,1,0,2:T(2,128)(2,1)} %copy.26), calls=%async_computation.1 | async-start | bytes 8388608 | tf_op jit(solution)/shard_map/all_to_all | solution.py:34
Sparse Core Ops, SparseCore 0:
  8.9 37.5 all-gather.1
where the time goes:
time: 182 us; the launch traced here: 181 us
  waiting for transfers between devices  85.6 us (47%)
  matrix products  45.6 us (25%)
  other arithmetic  16.5 us (9%)
  between operations  13.5 us (7%)
  local copies, waits for them, and re-layouts  11.6 us (6%)
  starting transfers between devices  8.48 us (5%)
    all_to_all x1, waiting for transfers between devices, local_step(): lax.all_to_all(part_out, 'dcp', 2, 2, tiled=True)  46.8 us
    all_gather x1, waiting for transfers between devices, local_step(): q_all = lax.all_gather(q_blk, 'dcp', axis=2, tiled=True)  38.1 us
    dot_general x1, matrix products, local_step(): jnp.einsum('bthd,bsd->bths', q_all, local_keys, preferred_element_type=jn...  25.4 us
    dot_general x1, matrix products, local_step(): jnp.einsum('bths,bsc->bthc', weights.astype(jnp.bfloat16), local_keys[:,...  20.2 us
    convert_element_type x1, local copies, waits for them, and re-layouts, local_step(): part_out = (part_out / row_sum[..., None]).astype(jnp.bfloat16)  8.43 us
    reduce_sum x1, other arithmetic, local_step(): row_sum = jnp.sum(weights, axis=-1)  8.07 us
    reduce_sum x1, other arithmetic, local_step(): merged = jnp.sum(merge_w[..., None] * recv_out.astype(jnp.float32), axis=2)  6.66 us
    all_to_all x1, starting transfers between devices, local_step(): lax.all_to_all(part_out, 'dcp', 2, 2, tiled=True)  4.95 us
  transfers between devices with their start and end apart: 3, of which 2 were waited for; matrix products, arithmetic and copies ran while one was open for 17% of the time, Pallas kernels for 0%

commit v1 on v0

v1 whole, which is shorter than its diff:
```python
import functools
import math

import jax
import jax.numpy as jnp
from jax import lax
from jax.experimental import pallas as pl
from jax.experimental.pallas import tpu as pltpu
from jax.sharding import PartitionSpec as P

LATENT = 512
ROPE = 64
NOPE = 128
PAGE = 64
CORES = 2
CHUNK = 4
KV_SLOTS = 4
AHEAD = 3
LANES = 128


def wide(col, n):
    return jnp.concatenate([col] * (n // LANES), axis=1)


def merge(o_a, l_a, o_b, l_b):
    top = jnp.maximum(l_a, l_b)
    e_a = jnp.exp(l_a - top)
    e_b = jnp.exp(l_b - top)
    total = e_a + e_b
    inv = 1.0 / total
    n = o_a.shape[1]
    return o_a * wide(e_a * inv, n) + o_b * wide(e_b * inv, n), top + jnp.log(total)


def kernel(group, rounds, min_rounds, len_ref, q_hbm, kv_hbm, out_ref, q_all, kv_buf, rank, own_o, own_l, sib_o, sib_l,
           got_o, got_l, chip_o, chip_l, hop_o, hop_l, mid_o, mid_l, fin_o, fin_l,
           load_sem, kv_sem, q_send, q_recv, qs_send, qs_recv, s_send, s_recv, h_send, h_recv, f_send, f_recv):
    chunks, _, per, rows, width = q_all.shape
    half = per // 2
    keys = kv_buf.shape[2]
    chips = group // CORES
    side = chips * rows
    me = lax.axis_index('dcp')
    chip, core = me // CORES, me % CORES
    right = lax.rem(chip + 1, chips) * CORES + core
    left = lax.rem(chip + chips - 1, chips) * CORES + core
    twin = chip * CORES + (CORES - 1 - core)
    scale = (NOPE + ROPE) ** -0.5

    def remote(src, dst, send, recv, to):
        return pltpu.make_async_remote_copy(src_ref=src, dst_ref=dst, send_sem=send, recv_sem=recv,
                                            device_id={'dcp': to}, device_id_type=pl.DeviceIdType.MESH)

    def q_copy(c, kind):
        if kind == 0:
            src, dst, to = q_all.at[c, 0], q_all.at[c, 1], right
        elif kind == 1:
            src, dst, to = q_all.at[c, 0], q_all.at[c, 2], left
        elif kind == 2:
            src, dst, to = q_all.at[c, 1, pl.ds(0, half)], q_all.at[c, 3, pl.ds(0, half)], right
        else:
            src, dst, to = q_all.at[c, 2, pl.ds(half, half)], q_all.at[c, 3, pl.ds(half, half)], left
        return remote(src, dst, q_send.at[c, kind], q_recv.at[c, kind], to)

    def q_twin(c):
        return remote(q_all.at[c, pl.ds(0, chips)], q_all.at[c, pl.ds(chips, chips)], qs_send.at[c], qs_recv.at[c], twin)

    def part_twin(c, what):
        src, dst = ((sib_o, got_o), (sib_l, got_l))[what]
        return remote(src.at[c], dst.at[c], s_send.at[c, what], s_recv.at[c, what], twin)

    def hop_copy(c, h, what):
        src = (chip_o.at[c, h, 3], chip_l.at[c, h])[what]
        dst = (hop_o.at[c, h], hop_l.at[c, h])[what]
        return remote(src, dst, h_send.at[c, h, what], h_recv.at[c, h, what], (right, left)[h])

    def fin_copy(c, s, h, what):
        if s == h:
            src = (mid_o.at[c, h], mid_l.at[c, h])[what]
        else:
            src = (chip_o.at[c, h, 2 - s], chip_l.at[c, h])[what]
        dst = (fin_o.at[c, s, h], fin_l.at[c, s, h])[what]
        return remote(src, dst, f_send.at[c, s, h, what], f_recv.at[c, s, h, what], (right, left)[s])

    def kv_copy(c, b):
        slot = lax.rem(c, KV_SLOTS)
        return pltpu.make_async_copy(kv_hbm.at[c * per + b], kv_buf.at[slot, b], kv_sem.at[slot, b])

    load = pltpu.make_async_copy(q_hbm, q_all.at[:, 0], load_sem)
    load.start()
    for c in range(min(KV_SLOTS, chunks)):
        for b in range(per):
            kv_copy(c, b).start()

    barrier = pltpu.get_barrier_semaphore()
    for peer in (left, right, twin):
        pl.semaphore_signal(barrier, inc=1, device_id={'dcp': peer}, device_id_type=pl.DeviceIdType.MESH)

    r_id = lax.broadcasted_iota(jnp.int32, (rows, keys), 0)
    k_id = lax.broadcasted_iota(jnp.int32, (rows, keys), 1)
    tokens = 2
    rank[...] = (k_id // PAGE * group + me) * PAGE + k_id % PAGE - r_id // (rows // tokens)

    load.wait()
    pl.semaphore_wait(barrier, 3)
    for c in range(min(AHEAD, chunks)):
        for kind in (0, 1):
            q_copy(c, kind).start()

    free_keys = (min_rounds * PAGE) // LANES * LANES

    def attend(c):
        slot = lax.rem(c, KV_SLOTS)
        for b in range(per):
            kv_copy(c, b).wait()
        for b in range(per):
            q = q_all[c, :, b].reshape(group * rows, width)
            kv = kv_buf.at[slot, b]
            s = lax.dot_general(q, kv[...], (((1,), (1,)), ((), ())), preferred_element_type=jnp.float32)
            tail = s[:, free_keys:].reshape(group, rows, keys - free_keys)
            limit = len_ref[c * per + b] - tokens
            seen = jnp.broadcast_to(rank[:, free_keys:][None], tail.shape) <= limit
            tail = jnp.where(seen, tail, -jnp.inf).reshape(group * rows, keys - free_keys)
            s = jnp.concatenate([s[:, :free_keys], tail], axis=1)
            top = jnp.max(s, axis=1, keepdims=True)
            p = jnp.exp2((s - top) * (scale * math.log2(math.e)))
            total = jnp.sum(p, axis=1, keepdims=True)
            o = jnp.dot(p.astype(jnp.bfloat16), kv[:, :LATENT], preferred_element_type=jnp.float32)
            o = o * (1.0 / total)
            lse = jnp.broadcast_to(top * scale + jnp.log(total), (group * rows, LANES))
            own_o[b] = o[:side]
            own_l[b] = lse[:side]
            sib_o[c, b] = o[side:].astype(jnp.bfloat16)
            sib_l[c, b] = lse[side:]

    lane_s = lax.broadcasted_iota(jnp.int32, (side, LANES), 1)
    row_s = lax.broadcasted_iota(jnp.int32, (side, LANES), 0)
    block = half * rows
    lane_b = lax.broadcasted_iota(jnp.int32, (block, LANES), 1)
    row_b = lax.broadcasted_iota(jnp.int32, (block, LANES), 0)

    def column(row, slot):
        picked = jnp.where(lane_b == row_b + slot * block, jnp.broadcast_to(row, (block, LANES)), 0.0)
        return jnp.broadcast_to(jnp.sum(picked, axis=1, keepdims=True), (block, LANES))

    def join_cores(c):
        for h in range(2):
            packed = jnp.zeros((1, LANES), jnp.float32)
            for n in range(half):
                b = h * half + n
                o, lse = merge(own_o[b], own_l[b], got_o[c, b].astype(jnp.float32), got_l[c, b])
                o = o.astype(jnp.bfloat16)
                for slot in range(chips):
                    chip_o[c, h, slot, n * rows:(n + 1) * rows] = o[slot * rows:(slot + 1) * rows]
                at = row_s // rows * block + n * rows + row_s % rows
                packed = packed + jnp.sum(jnp.where(lane_s == at, lse, 0.0), axis=0, keepdims=True)
            chip_l[c, h] = packed

    def join_hop(c):
        for h in range(2):
            slot = 2 - h
            row = chip_l[c, h]
            o, lse = merge(chip_o[c, h, slot].astype(jnp.float32), column(row, slot),
                           hop_o[c, h].astype(jnp.float32), column(hop_l[c, h], 3))
            mid_o[c, h] = o.astype(jnp.bfloat16)
            mid_l[c, h] = jnp.sum(jnp.where(lane_b == row_b + slot * block, lse, 0.0), axis=0, keepdims=True)

    def join_last(c):
        for h in range(2):
            parts = [(chip_o[c, h, 0], column(chip_l[c, h], 0))]
            for s in range(2):
                parts.append((fin_o[c, s, h], column(fin_l[c, s, h], 2 - s)))
            top = functools.reduce(jnp.maximum, [l for _, l in parts])
            weights = [jnp.exp(l - top) for _, l in parts]
            inv = 1.0 / functools.reduce(jnp.add, weights)
            o = functools.reduce(jnp.add, [part.astype(jnp.float32) * wide(w * inv, LATENT) for (part, _), w in zip(parts, weights)])
            o = o.astype(jnp.bfloat16)
            for n in range(half):
                out_ref[c * per + h * half + n] = o[n * rows:(n + 1) * rows]

    def stage(t, lag, fn):
        c = t - lag

        @pl.when(jnp.logical_and(c >= 0, c < chunks))
        def _():
            fn(c)

    def spread(c):
        for kind in (0, 1):
            q_copy(c, kind).wait_recv()
        for kind in (2, 3):
            q_copy(c, kind).start()

    def to_twin(c):
        for kind in (2, 3):
            q_copy(c, kind).wait_recv()
        q_twin(c).start()

    def send_own(c):
        for kind in (0, 1):
            q_copy(c, kind).start()

    def cores(c):
        for what in range(2):
            part_twin(c, what).wait_recv()
        join_cores(c)
        for what in range(2):
            for h in range(2):
                hop_copy(c, h, what).start()
            for s in range(2):
                fin_copy(c, s, 1 - s, what).start()

    def hop(c):
        for what in range(2):
            for h in range(2):
                hop_copy(c, h, what).wait_recv()
        join_hop(c)
        for what in range(2):
            for s in range(2):
                fin_copy(c, s, s, what).start()

    def last(c):
        for what in range(2):
            for s in range(2):
                for h in range(2):
                    fin_copy(c, s, h, what).wait_recv()
        join_last(c)

    def work(c):
        q_twin(c).wait_recv()
        attend(c)
        for what in range(2):
            part_twin(c, what).start()

        @pl.when(c + KV_SLOTS < chunks)
        def _():
            for b in range(per):
                kv_copy(c + KV_SLOTS, b).start()

    def step(t, carry):
        stage(t, -AHEAD, send_own)
        stage(t, 0, spread)
        stage(t, 1, to_twin)
        stage(t, 3, cores)
        stage(t, 4, hop)
        stage(t, 5, last)
        stage(t, 2, work)
        return carry

    lax.fori_loop(0, chunks + 5, step, 0)

    def drain(c, carry):
        for kind in range(4):
            q_copy(c, kind).wait_send()
        q_twin(c).wait_send()
        for what in range(2):
            part_twin(c, what).wait_send()
            for h in range(2):
                hop_copy(c, h, what).wait_send()
                for s in range(2):
                    fin_copy(c, s, h, what).wait_send()
        return carry

    lax.fori_loop(0, chunks, drain, 0)


def solution(mesh):
    group = mesh.shape['dcp']
    chips = group // CORES

    def local_step(q_blk, kv_blk, len_blk):
        batch, tokens, heads, width = q_blk.shape
        rounds = kv_blk.shape[1]
        keys = rounds * PAGE
        rows = tokens * heads
        chunks = batch // CHUNK
        half = CHUNK // 2
        block = half * rows
        side = chips * rows
        bf, f32 = jnp.bfloat16, jnp.float32
        scratch = [
            pltpu.VMEM((chunks, group, CHUNK, rows, width), bf),
            pltpu.VMEM((KV_SLOTS, CHUNK, keys, width), bf),
            pltpu.VMEM((rows, keys), jnp.int32),
            pltpu.VMEM((CHUNK, side, LATENT), f32),
            pltpu.VMEM((CHUNK, side, LANES), f32),
            pltpu.VMEM((chunks, CHUNK, side, LATENT), bf),
            pltpu.VMEM((chunks, CHUNK, side, LANES), f32),
            pltpu.VMEM((chunks, CHUNK, side, LATENT), bf),
            pltpu.VMEM((chunks, CHUNK, side, LANES), f32),
            pltpu.VMEM((chunks, 2, chips, block, LATENT), bf),
            pltpu.VMEM((chunks, 2, 1, LANES), f32),
            pltpu.VMEM((chunks, 2, block, LATENT), bf),
            pltpu.VMEM((chunks, 2, 1, LANES), f32),
            pltpu.VMEM((chunks, 2, block, LATENT), bf),
            pltpu.VMEM((chunks, 2, 1, LANES), f32),
            pltpu.VMEM((chunks, 2, 2, block, LATENT), bf),
            pltpu.VMEM((chunks, 2, 2, 1, LANES), f32),
            pltpu.SemaphoreType.DMA,
            pltpu.SemaphoreType.DMA((KV_SLOTS, CHUNK)),
        ]
        for shape in ((chunks, 4), (chunks,), (chunks, 2), (chunks, 2, 2), (chunks, 2, 2, 2)):
            scratch += [pltpu.SemaphoreType.DMA(shape)] * 2
        flops = 2 * batch * group * rows * keys * (width + LATENT)
        o = pl.pallas_call(
            functools.partial(kernel, group, rounds, rounds // 2 - 1),
            out_shape=jax.ShapeDtypeStruct((batch, rows, LATENT), bf),
            in_specs=[pl.BlockSpec(memory_space=pltpu.SMEM), pl.BlockSpec(memory_space=pl.ANY), pl.BlockSpec(memory_space=pl.ANY)],
            out_specs=pl.BlockSpec(memory_space=pltpu.VMEM),
            scratch_shapes=scratch,
            compiler_params=pltpu.CompilerParams(collective_id=0, has_side_effects=True, vmem_limit_bytes=62 * 2**20),
            cost_estimate=pl.CostEstimate(flops=flops, bytes_accessed=kv_blk.size * 2, transcendentals=batch * group * rows * keys),
        )(len_blk, q_blk.reshape(chunks, CHUNK, rows, width), kv_blk.reshape(batch, keys, width))
        return o.reshape(batch, tokens, heads, LATENT)

    return jax.shard_map(local_step, mesh=mesh, in_specs=(P('dp', None, 'dcp', None), P('dp', None, 'dcp', None, None), P('dp')), out_specs=P('dp', None, 'dcp', None), check_vma=False)
```

time: 182 us -> 78.4 us (0.43)
  the two profiles are of different devices: /device:TPU:81 before, /device:TPU:120 now
where the time goes in v1:
time: 78.4 us; the launch traced here: 78.2 us
  Pallas kernels  76.4 us (97%)
  local copies, waits for them, and re-layouts  1.87 us (2%)
    pallas_call x1, Pallas kernels, local_step(): pl.pallas_call(functools.partial(kernel, group, rounds, rounds // 2 - 1),...  76.4 us
    unnamed x1, local copies, waits for them, and re-layouts  1.87 us

profile of v1, /device:TPU:120, one launch (start us, length us, event | category | flops | bytes accessed | tf_op | source)
XLA Modules:
  0.0 78.2 jit_solution(14822752280353459483)
XLA Ops:
  0.0 76.4 %shard_map.37 = bf16[32,16,512]{2,1,0:T(8,128)(2,1)} custom-call(s32[32]{0:T(128)} %len_ref.1, bf16[8,4,16,576]{3,2,1,0:T(8,128)(2,1)} %bitcast.5, bf16[32,1024,576]{2,1,0:T(8,128)(2,1)} %bitcast.3), custom_call_target="tpu_custom_call" | custom-call | flops 9126805504 | bytes 37748736 | tf_op jit(solution)/shard_map/pallas_call | solution.py:306
  76.4 1.9 %copy.5 = bf16[32,2,8,512]{3,2,1,0:T(8,128)(2,1)} copy(bf16[32,2,8,512]{3,2,1,0:T(8,128)(2,1)} %bitcast.4) | data formatting | bytes 1048576

commit v2 on v1

v2 whole, which is shorter than its diff:
```python
import functools
import math

import jax
import jax.numpy as jnp
from jax import lax
from jax.experimental import pallas as pl
from jax.experimental.pallas import tpu as pltpu
from jax.sharding import PartitionSpec as P

LATENT = 512
ROPE = 64
NOPE = 128
PAGE = 64
CORES = 2
CHUNK = 2
KV_SLOTS = 8
AHEAD = 4
LAG = 2
KEPT = LAG
LANES = 128


def wide(col, n):
    return jnp.concatenate([col] * (n // LANES), axis=1)


def merge(o_a, l_a, o_b, l_b):
    top = jnp.maximum(l_a, l_b)
    e_a = jnp.exp(l_a - top)
    e_b = jnp.exp(l_b - top)
    total = e_a + e_b
    inv = 1.0 / total
    n = o_a.shape[1]
    return o_a * wide(e_a * inv, n) + o_b * wide(e_b * inv, n), top + jnp.log(total)


def kernel(group, min_rounds, len_ref, q_hbm, kv_hbm, out_ref, q_all, kv_buf, rank, own_o, own_l, sib_o, sib_l,
           got_o, got_l, chip_o, chip_l, hop_o, hop_l, mid_o, mid_l, fin_o, fin_l,
           load_sem, kv_sem, q_send, q_recv, s_send, s_recv, h_send, h_recv, f_send, f_recv):
    chunks, _, per, rows, width = q_all.shape
    keys = kv_buf.shape[2]
    chips = group // CORES
    side = chips * rows
    block = per * rows
    me = lax.axis_index('dcp')
    chip, core = me // CORES, me % CORES
    right = lax.rem(chip + 1, chips) * CORES + core
    left = lax.rem(chip + chips - 1, chips) * CORES + core
    twin = chip * CORES + (CORES - 1 - core)
    scale = (NOPE + ROPE) ** -0.5

    def remote(src, dst, send, recv, to):
        return pltpu.make_async_remote_copy(src_ref=src, dst_ref=dst, send_sem=send, recv_sem=recv,
                                            device_id={'dcp': to}, device_id_type=pl.DeviceIdType.MESH)

    def way(c):
        return lax.rem(c, 2)

    def toward(d):
        return jnp.where(d == 0, right, left)

    def q_copy(c, kind):
        if kind == 0:
            src, dst, to = q_all.at[c, 0], q_all.at[c, 1], right
        elif kind == 1:
            src, dst, to = q_all.at[c, 0], q_all.at[c, 2], left
        elif kind == 2:
            src, dst, to = q_all.at[c, 1 + way(c)], q_all.at[c, 3], toward(way(c))
        else:
            src, dst, to = q_all.at[c, pl.ds(0, chips)], q_all.at[c, pl.ds(chips, chips)], twin
        return remote(src, dst, q_send.at[c, kind], q_recv.at[c, kind], to)

    def part_twin(c, what):
        src, dst = ((sib_o, got_o), (sib_l, got_l))[what]
        return remote(src.at[c], dst.at[c], s_send.at[c, what], s_recv.at[c, what], twin)

    def hop_copy(c, what):
        src = (chip_o.at[c, 3], chip_l.at[c])[what]
        dst = (hop_o.at[c], hop_l.at[c])[what]
        return remote(src, dst, h_send.at[c, what], h_recv.at[c, what], toward(way(c)))

    def fin_copy(c, kind, what):
        if kind == 0:
            src, to = (mid_o.at[c], mid_l.at[c])[what], toward(way(c))
        else:
            src, to = (chip_o.at[c, 1 + way(c)], chip_l.at[c])[what], toward(1 - way(c))
        dst = (fin_o.at[c, kind], fin_l.at[c, kind])[what]
        return remote(src, dst, f_send.at[c, kind, what], f_recv.at[c, kind, what], to)

    def kv_copy(c, b):
        slot = lax.rem(c, KV_SLOTS)
        return pltpu.make_async_copy(kv_hbm.at[c * per + b], kv_buf.at[slot, b], kv_sem.at[slot, b])

    load = pltpu.make_async_copy(q_hbm, q_all.at[:, 0], load_sem)
    load.start()
    for c in range(min(KV_SLOTS, chunks)):
        for b in range(per):
            kv_copy(c, b).start()

    barrier = pltpu.get_barrier_semaphore()
    for peer in (left, right, twin):
        pl.semaphore_signal(barrier, inc=1, device_id={'dcp': peer}, device_id_type=pl.DeviceIdType.MESH)

    r_id = lax.broadcasted_iota(jnp.int32, (rows, keys), 0)
    k_id = lax.broadcasted_iota(jnp.int32, (rows, keys), 1)
    tokens = 2
    rank[...] = (k_id // PAGE * group + me) * PAGE + k_id % PAGE - r_id // (rows // tokens)

    load.wait()
    pl.semaphore_wait(barrier, 3)
    for c in range(min(AHEAD, chunks)):
        for kind in (0, 1):
            q_copy(c, kind).start()

    free_keys = (min_rounds * PAGE) // LANES * LANES

    def attend(c):
        slot = lax.rem(c, KV_SLOTS)
        for b in range(per):
            kv_copy(c, b).wait()
        for b in range(per):
            q = q_all[c, :, b].reshape(group * rows, width)
            kv = kv_buf.at[slot, b]
            s = lax.dot_general(q, kv[...], (((1,), (1,)), ((), ())), preferred_element_type=jnp.float32)
            tail = s[:, free_keys:].reshape(group, rows, keys - free_keys)
            limit = len_ref[c * per + b] - tokens
            seen = jnp.broadcast_to(rank[:, free_keys:][None], tail.shape) <= limit
            tail = jnp.where(seen, tail, -jnp.inf).reshape(group * rows, keys - free_keys)
            s = jnp.concatenate([s[:, :free_keys], tail], axis=1)
            top = jnp.max(s, axis=1, keepdims=True)
            p = jnp.exp2((s - top) * (scale * math.log2(math.e)))
            total = jnp.sum(p, axis=1, keepdims=True)
            o = jnp.dot(p.astype(jnp.bfloat16), kv[:, :LATENT], preferred_element_type=jnp.float32)
            o = o * (1.0 / total)
            lse = jnp.broadcast_to(top * scale + jnp.log(total), (group * rows, LANES))
            keep = lax.rem(c, KEPT)
            own_o[keep, b] = o[:side]
            own_l[keep, b] = lse[:side]
            sib_o[c, b] = o[side:].astype(jnp.bfloat16)
            sib_l[c, b] = lse[side:]

    lane_s = lax.broadcasted_iota(jnp.int32, (side, LANES), 1)
    row_s = lax.broadcasted_iota(jnp.int32, (side, LANES), 0)
    lane_b = lax.broadcasted_iota(jnp.int32, (block, LANES), 1)
    row_b = lax.broadcasted_iota(jnp.int32, (block, LANES), 0)

    def column(row, slot):
        picked = jnp.where(lane_b == row_b + slot * block, jnp.broadcast_to(row, (block, LANES)), 0.0)
        return jnp.broadcast_to(jnp.sum(picked, axis=1, keepdims=True), (block, LANES))

    def join_cores(c):
        packed = jnp.zeros((1, LANES), jnp.float32)
        keep = lax.rem(c, KEPT)
        for b in range(per):
            o, lse = merge(own_o[keep, b], own_l[keep, b], got_o[c, b].astype(jnp.float32), got_l[c, b])
            o = o.astype(jnp.bfloat16)
            for slot in range(chips):
                chip_o[c, slot, b * rows:(b + 1) * rows] = o[slot * rows:(slot + 1) * rows]
            at = row_s // rows * block + b * rows + row_s % rows
            packed = packed + jnp.sum(jnp.where(lane_s == at, lse, 0.0), axis=0, keepdims=True)
        chip_l[c] = packed

    def join_hop(c):
        slot = 2 - way(c)
        o, lse = merge(chip_o[c, slot].astype(jnp.float32), column(chip_l[c], slot), hop_o[c].astype(jnp.float32), column(hop_l[c], 3))
        mid_o[c] = o.astype(jnp.bfloat16)
        mid_l[c] = jnp.sum(jnp.where(lane_b == row_b, lse, 0.0), axis=0, keepdims=True)

    def join_last(c):
        parts = [(chip_o[c, 0], column(chip_l[c], 0)), (fin_o[c, 0], column(fin_l[c, 0], 0)),
                 (fin_o[c, 1], column(fin_l[c, 1], 1 + way(c)))]
        top = functools.reduce(jnp.maximum, [l for _, l in parts])
        weights = [jnp.exp(l - top) for _, l in parts]
        inv = 1.0 / functools.reduce(jnp.add, weights)
        o = functools.reduce(jnp.add, [part.astype(jnp.float32) * wide(w * inv, LATENT) for (part, _), w in zip(parts, weights)])
        o = o.astype(jnp.bfloat16)
        for b in range(per):
            out_ref[c * per + b] = o[b * rows:(b + 1) * rows]

    def stage(t, lag, fn):
        c = t - lag

        @pl.when(jnp.logical_and(c >= 0, c < chunks))
        def _():
            fn(c)

    def send_own(c):
        for kind in (0, 1):
            q_copy(c, kind).start()

    def spread(c):
        for kind in (0, 1):
            q_copy(c, kind).wait_recv()
        q_copy(c, 2).start()

    def to_twin(c):
        q_copy(c, 2).wait_recv()
        q_copy(c, 3).start()

    def work(c):
        q_copy(c, 3).wait_recv()
        attend(c)
        for what in range(2):
            part_twin(c, what).start()

        @pl.when(c + KV_SLOTS < chunks)
        def _():
            for b in range(per):
                kv_copy(c + KV_SLOTS, b).start()

    def cores(c):
        for what in range(2):
            part_twin(c, what).wait_recv()
        join_cores(c)
        for what in range(2):
            hop_copy(c, what).start()
            fin_copy(c, 1, what).start()

    def hop(c):
        for what in range(2):
            hop_copy(c, what).wait_recv()
        join_hop(c)
        for what in range(2):
            fin_copy(c, 0, what).start()

    def last(c):
        for what in range(2):
            for kind in range(2):
                fin_copy(c, kind, what).wait_recv()
        join_last(c)

    def sent(c):
        for kind in range(4):
            q_copy(c, kind).wait_send()
        for what in range(2):
            part_twin(c, what).wait_send()
            hop_copy(c, what).wait_send()
            for kind in range(2):
                fin_copy(c, kind, what).wait_send()

    def step(t, carry):
        stage(t, -AHEAD, send_own)
        stage(t, 0, spread)
        stage(t, LAG, to_twin)
        stage(t, 3 * LAG, cores)
        stage(t, 4 * LAG, hop)
        stage(t, 5 * LAG, last)
        stage(t, 5 * LAG + 1, sent)
        stage(t, 2 * LAG, work)
        return carry

    lax.fori_loop(0, chunks + 5 * LAG + 1, step, 0)


def solution(mesh):
    group = mesh.shape['dcp']
    chips = group // CORES

    def local_step(q_blk, kv_blk, len_blk):
        batch, tokens, heads, width = q_blk.shape
        rounds = kv_blk.shape[1]
        keys = rounds * PAGE
        rows = tokens * heads
        chunks = batch // CHUNK
        block = CHUNK * rows
        side = chips * rows
        bf, f32 = jnp.bfloat16, jnp.float32
        scratch = [
            pltpu.VMEM((chunks, group, CHUNK, rows, width), bf),
            pltpu.VMEM((KV_SLOTS, CHUNK, keys, width), bf),
            pltpu.VMEM((rows, keys), jnp.int32),
            pltpu.VMEM((KEPT, CHUNK, side, LATENT), f32),
            pltpu.VMEM((KEPT, CHUNK, side, LANES), f32),
            pltpu.VMEM((chunks, CHUNK, side, LATENT), bf),
            pltpu.VMEM((chunks, CHUNK, side, LANES), f32),
            pltpu.VMEM((chunks, CHUNK, side, LATENT), bf),
            pltpu.VMEM((chunks, CHUNK, side, LANES), f32),
            pltpu.VMEM((chunks, chips, block, LATENT), bf),
            pltpu.VMEM((chunks, 1, LANES), f32),
            pltpu.VMEM((chunks, block, LATENT), bf),
            pltpu.VMEM((chunks, 1, LANES), f32),
            pltpu.VMEM((chunks, block, LATENT), bf),
            pltpu.VMEM((chunks, 1, LANES), f32),
            pltpu.VMEM((chunks, 2, block, LATENT), bf),
            pltpu.VMEM((chunks, 2, 1, LANES), f32),
            pltpu.SemaphoreType.DMA,
            pltpu.SemaphoreType.DMA((KV_SLOTS, CHUNK)),
        ]
        for shape in ((chunks, 4), (chunks, 2), (chunks, 2), (chunks, 2, 2)):
            scratch += [pltpu.SemaphoreType.DMA(shape)] * 2
        flops = 2 * batch * group * rows * keys * (width + LATENT)
        o = pl.pallas_call(
            functools.partial(kernel, group, rounds // 2 - 1),
            out_shape=jax.ShapeDtypeStruct((batch, rows, LATENT), bf),
            in_specs=[pl.BlockSpec(memory_space=pltpu.SMEM), pl.BlockSpec(memory_space=pl.ANY), pl.BlockSpec(memory_space=pl.ANY)],
            out_specs=pl.BlockSpec(memory_space=pltpu.VMEM),
            scratch_shapes=scratch,
            compiler_params=pltpu.CompilerParams(collective_id=0, has_side_effects=True, vmem_limit_bytes=62 * 2**20),
            cost_estimate=pl.CostEstimate(flops=flops, bytes_accessed=kv_blk.size * 2, transcendentals=batch * group * rows * keys),
        )(len_blk, q_blk.reshape(chunks, CHUNK, rows, width), kv_blk.reshape(batch, keys, width))
        return o.reshape(batch, tokens, heads, LATENT)

    return jax.shard_map(local_step, mesh=mesh, in_specs=(P('dp', None, 'dcp', None), P('dp', None, 'dcp', None, None), P('dp')), out_specs=P('dp', None, 'dcp', None), check_vma=False)
```

time: 78.4 us -> 69.4 us (0.89)
  the two profiles are of different devices: /device:TPU:120 before, /device:TPU:81 now
where the time goes in v2:
time: 69.4 us; the launch traced here: 69.3 us
  Pallas kernels  67.4 us (97%)
  local copies, waits for them, and re-layouts  1.87 us (3%)
    pallas_call x1, Pallas kernels, local_step(): pl.pallas_call(functools.partial(kernel, group, rounds // 2 - 1), out_sha...  67.4 us
    unnamed x1, local copies, waits for them, and re-layouts  1.87 us

profile of v2, /device:TPU:81, one launch (start us, length us, event | category | flops | bytes accessed | tf_op | source)
XLA Modules:
  0.0 69.3 jit_solution(7702193231876556349)
XLA Ops:
  0.0 67.4 %shard_map.37 = bf16[32,16,512]{2,1,0:T(8,128)(2,1)} custom-call(s32[32]{0:T(128)} %len_ref.1, bf16[16,2,16,576]{3,2,1,0:T(8,128)(2,1)} %bitcast.5, bf16[32,1024,576]{2,1,0:T(8,128)(2,1)} %bitcast.3), custom_call_target="tpu_custom_call" | custom-call | flops 9126805504 | bytes 37748736 | tf_op jit(solution)/shard_map/pallas_call | solution.py:293
  67.4 1.9 %copy.5 = bf16[32,2,8,512]{3,2,1,0:T(8,128)(2,1)} copy(bf16[32,2,8,512]{3,2,1,0:T(8,128)(2,1)} %bitcast.4) | data formatting | bytes 1048576

commit v3 on v2

--- a/solution.py
+++ b/solution.py
@@ -15,8 +15,8 @@
 CORES = 2
 CHUNK = 2
 KV_SLOTS = 8
-AHEAD = 4
-LAG = 2
+AHEAD = 6
+LAG = 3
 KEPT = LAG
 LANES = 128
 

time: 69.4 us -> 70.5 us (1.016); the launches traced: 69.3 us -> 69.3 us
  no operation moved by 1% of the time
where the time goes in v3:
time: 70.5 us; the launch traced here: 69.3 us
  Pallas kernels  67.5 us (96%)
  local copies, waits for them, and re-layouts  1.87 us (3%)
    pallas_call x1, Pallas kernels, local_step(): pl.pallas_call(functools.partial(kernel, group, rounds // 2 - 1), out_sha...  67.5 us
    unnamed x1, local copies, waits for them, and re-layouts  1.87 us

profile of v3, /device:TPU:81, one launch (start us, length us, event | category | flops | bytes accessed | tf_op | source)
XLA Modules:
  0.0 69.3 jit_solution(12790952395406133208)
XLA Ops:
  0.0 67.5 %shard_map.37 = bf16[32,16,512]{2,1,0:T(8,128)(2,1)} custom-call(s32[32]{0:T(128)} %len_ref.1, bf16[16,2,16,576]{3,2,1,0:T(8,128)(2,1)} %bitcast.5, bf16[32,1024,576]{2,1,0:T(8,128)(2,1)} %bitcast.3), custom_call_target="tpu_custom_call" | custom-call | flops 9126805504 | bytes 37748736 | tf_op jit(solution)/shard_map/pallas_call | solution.py:293
  67.5 1.9 %copy.5 = bf16[32,2,8,512]{3,2,1,0:T(8,128)(2,1)} copy(bf16[32,2,8,512]{3,2,1,0:T(8,128)(2,1)} %bitcast.4) | data formatting | bytes 1048576

commit v4 on v3

--- a/solution.py
+++ b/solution.py
@@ -13,11 +13,11 @@
 NOPE = 128
 PAGE = 64
 CORES = 2
-CHUNK = 2
-KV_SLOTS = 8
-AHEAD = 6
-LAG = 3
-KEPT = LAG
+CHUNK = 4
+KV_SLOTS = 4
+AHEAD = 3
+KEPT = 2
+SENDS = 4
 LANES = 128
 
 
@@ -43,6 +43,7 @@
     chips = group // CORES
     side = chips * rows
     block = per * rows
+    lot = LANES // block
     me = lax.axis_index('dcp')
     chip, core = me // CORES, me % CORES
     right = lax.rem(chip + 1, chips) * CORES + core
@@ -69,35 +70,43 @@
             src, dst, to = q_all.at[c, 1 + way(c)], q_all.at[c, 3], toward(way(c))
         else:
             src, dst, to = q_all.at[c, pl.ds(0, chips)], q_all.at[c, pl.ds(chips, chips)], twin
-        return remote(src, dst, q_send.at[c, kind], q_recv.at[c, kind], to)
+        return remote(src, dst, q_send.at[lax.rem(c, SENDS), kind], q_recv.at[c, kind], to)
 
     def part_twin(c, what):
         src, dst = ((sib_o, got_o), (sib_l, got_l))[what]
-        return remote(src.at[c], dst.at[c], s_send.at[c, what], s_recv.at[c, what], twin)
+        return remote(src.at[c], dst.at[c], s_send.at[lax.rem(c, SENDS), what], s_recv.at[c, what], twin)
 
     def hop_copy(c, what):
-        src = (chip_o.at[c, 3], chip_l.at[c])[what]
+        src = (chip_o.at[c, 3], chip_l.at[c, 3 // lot])[what]
         dst = (hop_o.at[c], hop_l.at[c])[what]
-        return remote(src, dst, h_send.at[c, what], h_recv.at[c, what], toward(way(c)))
+        return remote(src, dst, h_send.at[lax.rem(c, SENDS), what], h_recv.at[c, what], toward(way(c)))
 
     def fin_copy(c, kind, what):
         if kind == 0:
             src, to = (mid_o.at[c], mid_l.at[c])[what], toward(way(c))
         else:
-            src, to = (chip_o.at[c, 1 + way(c)], chip_l.at[c])[what], toward(1 - way(c))
+            slot = 1 + way(c)
+            src, to = (chip_o.at[c, slot], chip_l.at[c, slot // lot])[what], toward(1 - way(c))
         dst = (fin_o.at[c, kind], fin_l.at[c, kind])[what]
-        return remote(src, dst, f_send.at[c, kind, what], f_recv.at[c, kind, what], to)
+        return remote(src, dst, f_send.at[lax.rem(c, SENDS), kind, what], f_recv.at[c, kind, what], to)
 
     def kv_copy(c, b):
         slot = lax.rem(c, KV_SLOTS)
         return pltpu.make_async_copy(kv_hbm.at[c * per + b], kv_buf.at[slot, b], kv_sem.at[slot, b])
 
+    def go(make, c, *which):
+        @pl.when(c >= SENDS)
+        def _():
+            make(c - SENDS, *which).wait_send()
+
+        make(c, *which).start()
+
+    def send_own(c):
+        for kind in (0, 1):
+            go(q_copy, c, kind)
+
     load = pltpu.make_async_copy(q_hbm, q_all.at[:, 0], load_sem)
     load.start()
-    for c in range(min(KV_SLOTS, chunks)):
-        for b in range(per):
-            kv_copy(c, b).start()
-
     barrier = pltpu.get_barrier_semaphore()
     for peer in (left, right, twin):
         pl.semaphore_signal(barrier, inc=1, device_id={'dcp': peer}, device_id_type=pl.DeviceIdType.MESH)
@@ -110,8 +119,10 @@
     load.wait()
     pl.semaphore_wait(barrier, 3)
     for c in range(min(AHEAD, chunks)):
-        for kind in (0, 1):
-            q_copy(c, kind).start()
+        send_own(jnp.int32(c))
+    for c in range(min(KV_SLOTS, chunks)):
+        for b in range(per):
+            kv_copy(c, b).start()
 
     free_keys = (min_rounds * PAGE) // LANES * LANES
 
@@ -140,17 +151,17 @@
             sib_o[c, b] = o[side:].astype(jnp.bfloat16)
             sib_l[c, b] = lse[side:]
 
-    lane_s = lax.broadcasted_iota(jnp.int32, (side, LANES), 1)
-    row_s = lax.broadcasted_iota(jnp.int32, (side, LANES), 0)
+    lane_s = lax.broadcasted_iota(jnp.int32, (lot * rows, LANES), 1)
+    row_s = lax.broadcasted_iota(jnp.int32, (lot * rows, LANES), 0)
     lane_b = lax.broadcasted_iota(jnp.int32, (block, LANES), 1)
     row_b = lax.broadcasted_iota(jnp.int32, (block, LANES), 0)
 
     def column(row, slot):
-        picked = jnp.where(lane_b == row_b + slot * block, jnp.broadcast_to(row, (block, LANES)), 0.0)
+        picked = jnp.where(lane_b == row_b + lax.rem(slot, lot) * block, jnp.broadcast_to(row, (block, LANES)), 0.0)
         return jnp.broadcast_to(jnp.sum(picked, axis=1, keepdims=True), (block, LANES))
 
     def join_cores(c):
-        packed = jnp.zeros((1, LANES), jnp.float32)
+        packed = [jnp.zeros((1, LANES), jnp.float32) for _ in range(chips // lot)]
         keep = lax.rem(c, KEPT)
         for b in range(per):
             o, lse = merge(own_o[keep, b], own_l[keep, b], got_o[c, b].astype(jnp.float32), got_l[c, b])
@@ -158,17 +169,21 @@
             for slot in range(chips):
                 chip_o[c, slot, b * rows:(b + 1) * rows] = o[slot * rows:(slot + 1) * rows]
             at = row_s // rows * block + b * rows + row_s % rows
-            packed = packed + jnp.sum(jnp.where(lane_s == at, lse, 0.0), axis=0, keepdims=True)
-        chip_l[c] = packed
+            for j in range(chips // lot):
+                part = lse[j * lot * rows:(j + 1) * lot * rows]
+                packed[j] = packed[j] + jnp.sum(jnp.where(lane_s == at, part, 0.0), axis=0, keepdims=True)
+        for j in range(chips // lot):
+            chip_l[c, j] = packed[j]
 
     def join_hop(c):
         slot = 2 - way(c)
-        o, lse = merge(chip_o[c, slot].astype(jnp.float32), column(chip_l[c], slot), hop_o[c].astype(jnp.float32), column(hop_l[c], 3))
+        o, lse = merge(chip_o[c, slot].astype(jnp.float32), column(chip_l[c, slot // lot], slot),
+                       hop_o[c].astype(jnp.float32), column(hop_l[c], jnp.int32(3)))
         mid_o[c] = o.astype(jnp.bfloat16)
         mid_l[c] = jnp.sum(jnp.where(lane_b == row_b, lse, 0.0), axis=0, keepdims=True)
 
     def join_last(c):
-        parts = [(chip_o[c, 0], column(chip_l[c], 0)), (fin_o[c, 0], column(fin_l[c, 0], 0)),
+        parts = [(chip_o[c, 0], column(chip_l[c, 0], jnp.int32(0))), (fin_o[c, 0], column(fin_l[c, 0], jnp.int32(0))),
                  (fin_o[c, 1], column(fin_l[c, 1], 1 + way(c)))]
         top = functools.reduce(jnp.maximum, [l for _, l in parts])
         weights = [jnp.exp(l - top) for _, l in parts]
@@ -185,24 +200,20 @@
         def _():
             fn(c)
 
-    def send_own(c):
-        for kind in (0, 1):
-            q_copy(c, kind).start()
-
     def spread(c):
         for kind in (0, 1):
             q_copy(c, kind).wait_recv()
-        q_copy(c, 2).start()
+        go(q_copy, c, 2)
 
     def to_twin(c):
         q_copy(c, 2).wait_recv()
-        q_copy(c, 3).start()
+        go(q_copy, c, 3)
 
     def work(c):
         q_copy(c, 3).wait_recv()
         attend(c)
         for what in range(2):
-            part_twin(c, what).start()
+            go(part_twin, c, what)
 
         @pl.when(c + KV_SLOTS < chunks)
         def _():
@@ -214,15 +225,15 @@
             part_twin(c, what).wait_recv()
         join_cores(c)
         for what in range(2):
-            hop_copy(c, what).start()
-            fin_copy(c, 1, what).start()
+            go(hop_copy, c, what)
+            go(fin_copy, c, 1, what)
 
     def hop(c):
         for what in range(2):
             hop_copy(c, what).wait_recv()
         join_hop(c)
         for what in range(2):
-            fin_copy(c, 0, what).start()
+            go(fin_copy, c, 0, what)
 
     def last(c):
         for what in range(2):
@@ -230,7 +241,19 @@
                 fin_copy(c, kind, what).wait_recv()
         join_last(c)
 
-    def sent(c):
+    def step(t, carry):
+        stage(t, -AHEAD, send_own)
+        stage(t, 0, spread)
+        stage(t, 1, to_twin)
+        stage(t, 4, cores)
+        stage(t, 6, hop)
+        stage(t, 8, last)
+        stage(t, 2, work)
+        return carry
+
+    lax.fori_loop(0, chunks + 8, step, 0)
+    for c in range(max(chunks - SENDS, 0), chunks):
+        c = jnp.int32(c)
         for kind in range(4):
             q_copy(c, kind).wait_send()
         for what in range(2):
@@ -238,19 +261,6 @@
             hop_copy(c, what).wait_send()
             for kind in range(2):
                 fin_copy(c, kind, what).wait_send()
-
-    def step(t, carry):
-        stage(t, -AHEAD, send_own)
-        stage(t, 0, spread)
-        stage(t, LAG, to_twin)
-        stage(t, 3 * LAG, cores)
-        stage(t, 4 * LAG, hop)
-        stage(t, 5 * LAG, last)
-        stage(t, 5 * LAG + 1, sent)
-        stage(t, 2 * LAG, work)
-        return carry
-
-    lax.fori_loop(0, chunks + 5 * LAG + 1, step, 0)
 
 
 def solution(mesh):
@@ -277,7 +287,7 @@
             pltpu.VMEM((chunks, CHUNK, side, LATENT), bf),
             pltpu.VMEM((chunks, CHUNK, side, LANES), f32),
             pltpu.VMEM((chunks, chips, block, LATENT), bf),
-            pltpu.VMEM((chunks, 1, LANES), f32),
+            pltpu.VMEM((chunks, chips * block // LANES, 1, LANES), f32),
             pltpu.VMEM((chunks, block, LATENT), bf),
             pltpu.VMEM((chunks, 1, LANES), f32),
             pltpu.VMEM((chunks, block, LATENT), bf),
@@ -287,8 +297,8 @@
             pltpu.SemaphoreType.DMA,
             pltpu.SemaphoreType.DMA((KV_SLOTS, CHUNK)),
         ]
-        for shape in ((chunks, 4), (chunks, 2), (chunks, 2), (chunks, 2, 2)):
-            scratch += [pltpu.SemaphoreType.DMA(shape)] * 2
+        for shape in ((4,), (2,), (2,), (2, 2)):
+            scratch += [pltpu.SemaphoreType.DMA((SENDS, *shape)), pltpu.SemaphoreType.DMA((chunks, *shape))]
         flops = 2 * batch * group * rows * keys * (width + LATENT)
         o = pl.pallas_call(
             functools.partial(kernel, group, rounds // 2 - 1),

time: 70.5 us -> 63.1 us (0.90); the launches traced: 69.3 us -> 62.9 us
  Pallas kernels: 67.5 us -> 61.1 us
    pallas_call x1, Pallas kernels: 67.5 us -> 61.1 us  [local_step(): pl.pallas_call(functools.partial(kernel, group, rounds // 2 - 1), out_sha...]
where the time goes in v4:
time: 63.1 us; the launch traced here: 62.9 us
  Pallas kernels  61.1 us (97%)
  local copies, waits for them, and re-layouts  1.87 us (3%)
    pallas_call x1, Pallas kernels, local_step(): pl.pallas_call(functools.partial(kernel, group, rounds // 2 - 1), out_sha...  61.1 us
    unnamed x1, local copies, waits for them, and re-layouts  1.87 us

profile of v4, /device:TPU:81, one launch (start us, length us, event | category | flops | bytes accessed | tf_op | source)
XLA Modules:
  0.0 62.9 jit_solution(1578857997861654122)
XLA Ops:
  0.0 61.1 %shard_map.37 = bf16[32,16,512]{2,1,0:T(8,128)(2,1)} custom-call(s32[32]{0:T(128)} %len_ref.1, bf16[8,4,16,576]{3,2,1,0:T(8,128)(2,1)} %bitcast.5, bf16[32,1024,576]{2,1,0:T(8,128)(2,1)} %bitcast.3), custom_call_target="tpu_custom_call" | custom-call | flops 9126805504 | bytes 37748736 | tf_op jit(solution)/shard_map/pallas_call | solution.py:303
  61.1 1.9 %copy.5 = bf16[32,2,8,512]{3,2,1,0:T(8,128)(2,1)} copy(bf16[32,2,8,512]{3,2,1,0:T(8,128)(2,1)} %bitcast.4) | data formatting | bytes 1048576

commit v5 on v4

--- a/solution.py
+++ b/solution.py
@@ -13,10 +13,10 @@
 NOPE = 128
 PAGE = 64
 CORES = 2
-CHUNK = 4
-KV_SLOTS = 4
-AHEAD = 3
-KEPT = 2
+CHUNK = 2
+KV_SLOTS = 8
+AHEAD = 2
+KEPT = 4
 SENDS = 4
 LANES = 128
 
@@ -35,9 +35,8 @@
     return o_a * wide(e_a * inv, n) + o_b * wide(e_b * inv, n), top + jnp.log(total)
 
 
-def kernel(group, min_rounds, len_ref, q_hbm, kv_hbm, out_ref, q_all, kv_buf, rank, own_o, own_l, sib_o, sib_l,
-           got_o, got_l, chip_o, chip_l, hop_o, hop_l, mid_o, mid_l, fin_o, fin_l,
-           load_sem, kv_sem, q_send, q_recv, s_send, s_recv, h_send, h_recv, f_send, f_recv):
+def kernel(group, min_rounds, len_ref, q_hbm, kv_hbm, out_hbm, q_all, kv_buf, rank, own, sib, got, chip_o, chip_l, hop_o, hop_l, mid_o, mid_l, fin_o, fin_l,
+           out_buf, load_sem, kv_sem, out_sem, q_send, q_recv, s_send, s_recv, h_send, h_recv, f_send, f_recv):
     chunks, _, per, rows, width = q_all.shape
     keys = kv_buf.shape[2]
     chips = group // CORES
@@ -72,9 +71,8 @@
             src, dst, to = q_all.at[c, pl.ds(0, chips)], q_all.at[c, pl.ds(chips, chips)], twin
         return remote(src, dst, q_send.at[lax.rem(c, SENDS), kind], q_recv.at[c, kind], to)
 
-    def part_twin(c, what):
-        src, dst = ((sib_o, got_o), (sib_l, got_l))[what]
-        return remote(src.at[c], dst.at[c], s_send.at[lax.rem(c, SENDS), what], s_recv.at[c, what], twin)
+    def part_twin(c):
+        return remote(sib.at[c], got.at[c], s_send.at[lax.rem(c, SENDS)], s_recv.at[c], twin)
 
     def hop_copy(c, what):
         src = (chip_o.at[c, 3], chip_l.at[c, 3 // lot])[what]
@@ -90,6 +88,9 @@
         dst = (fin_o.at[c, kind], fin_l.at[c, kind])[what]
         return remote(src, dst, f_send.at[lax.rem(c, SENDS), kind, what], f_recv.at[c, kind, what], to)
 
+    def out_copy(c):
+        return pltpu.make_async_copy(out_buf.at[c], out_hbm.at[c], out_sem.at[lax.rem(c, SENDS)])
+
     def kv_copy(c, b):
         slot = lax.rem(c, KV_SLOTS)
         return pltpu.make_async_copy(kv_hbm.at[c * per + b], kv_buf.at[slot, b], kv_sem.at[slot, b])
@@ -126,30 +127,35 @@
 
     free_keys = (min_rounds * PAGE) // LANES * LANES
 
+    def scores(c, b):
+        q = q_all[c, :, b].reshape(group * rows, width)
+        s = lax.dot_general(q, kv_buf[lax.rem(c, KV_SLOTS), b], (((1,), (1,)), ((), ())), preferred_element_type=jnp.float32)
+        tail = s[:, free_keys:].reshape(group, rows, keys - free_keys)
+        limit = len_ref[c * per + b] - tokens
+        seen = jnp.broadcast_to(rank[:, free_keys:][None], tail.shape) <= limit
+        tail = jnp.where(seen, tail, -jnp.inf).reshape(group * rows, keys - free_keys)
+        return jnp.concatenate([s[:, :free_keys], tail], axis=1)
+
+    def values(c, b, s):
+        top = jnp.max(s, axis=1, keepdims=True)
+        p = jnp.exp2((s - top) * (scale * math.log2(math.e)))
+        total = jnp.sum(p, axis=1, keepdims=True)
+        o = jnp.dot(p.astype(jnp.bfloat16), kv_buf[lax.rem(c, KV_SLOTS), b, :, :LATENT], preferred_element_type=jnp.float32)
+        o = o * (1.0 / total)
+        lse = jnp.broadcast_to(top * scale + jnp.log(total), (group * rows, LANES))
+        keep = lax.rem(c, KEPT)
+        own[keep, b, :, :LATENT] = o[:side]
+        own[keep, b, :, LATENT:] = lse[:side]
+        sib[c, b, :, :LATENT] = o[side:]
+        sib[c, b, :, LATENT:] = lse[side:]
+
     def attend(c):
-        slot = lax.rem(c, KV_SLOTS)
+        ahead = scores(c, 0)
         for b in range(per):
-            kv_copy(c, b).wait()
-        for b in range(per):
-            q = q_all[c, :, b].reshape(group * rows, width)
-            kv = kv_buf.at[slot, b]
-            s = lax.dot_general(q, kv[...], (((1,), (1,)), ((), ())), preferred_element_type=jnp.float32)
-            tail = s[:, free_keys:].reshape(group, rows, keys - free_keys)
-            limit = len_ref[c * per + b] - tokens
-            seen = jnp.broadcast_to(rank[:, free_keys:][None], tail.shape) <= limit
-            tail = jnp.where(seen, tail, -jnp.inf).reshape(group * rows, keys - free_keys)
-            s = jnp.concatenate([s[:, :free_keys], tail], axis=1)
-            top = jnp.max(s, axis=1, keepdims=True)
-            p = jnp.exp2((s - top) * (scale * math.log2(math.e)))
-            total = jnp.sum(p, axis=1, keepdims=True)
-            o = jnp.dot(p.astype(jnp.bfloat16), kv[:, :LATENT], preferred_element_type=jnp.float32)
-            o = o * (1.0 / total)
-            lse = jnp.broadcast_to(top * scale + jnp.log(total), (group * rows, LANES))
-            keep = lax.rem(c, KEPT)
-            own_o[keep, b] = o[:side]
-            own_l[keep, b] = lse[:side]
-            sib_o[c, b] = o[side:].astype(jnp.bfloat16)
-            sib_l[c, b] = lse[side:]
+            now = ahead
+            if b + 1 < per:
+                ahead = scores(c, b + 1)
+            values(c, b, now)
 
     lane_s = lax.broadcasted_iota(jnp.int32, (lot * rows, LANES), 1)
     row_s = lax.broadcasted_iota(jnp.int32, (lot * rows, LANES), 0)
@@ -164,7 +170,7 @@
         packed = [jnp.zeros((1, LANES), jnp.float32) for _ in range(chips // lot)]
         keep = lax.rem(c, KEPT)
         for b in range(per):
-            o, lse = merge(own_o[keep, b], own_l[keep, b], got_o[c, b].astype(jnp.float32), got_l[c, b])
+            o, lse = merge(own[keep, b, :, :LATENT], own[keep, b, :, LATENT:], got[c, b, :, :LATENT], got[c, b, :, LATENT:])
             o = o.astype(jnp.bfloat16)
             for slot in range(chips):
                 chip_o[c, slot, b * rows:(b + 1) * rows] = o[slot * rows:(slot + 1) * rows]
@@ -191,7 +197,7 @@
         o = functools.reduce(jnp.add, [part.astype(jnp.float32) * wide(w * inv, LATENT) for (part, _), w in zip(parts, weights)])
         o = o.astype(jnp.bfloat16)
         for b in range(per):
-            out_ref[c * per + b] = o[b * rows:(b + 1) * rows]
+            out_buf[c, b] = o[b * rows:(b + 1) * rows]
 
     def stage(t, lag, fn):
         c = t - lag
@@ -209,58 +215,87 @@
         q_copy(c, 2).wait_recv()
         go(q_copy, c, 3)
 
-    def work(c):
-        q_copy(c, 3).wait_recv()
-        attend(c)
-        for what in range(2):
-            go(part_twin, c, what)
-
-        @pl.when(c + KV_SLOTS < chunks)
-        def _():
-            for b in range(per):
-                kv_copy(c + KV_SLOTS, b).start()
-
-    def cores(c):
-        for what in range(2):
-            part_twin(c, what).wait_recv()
-        join_cores(c)
+    def cores_in(c):
+        part_twin(c).wait_recv()
+
+    def cores_out(c):
         for what in range(2):
             go(hop_copy, c, what)
             go(fin_copy, c, 1, what)
 
-    def hop(c):
+    def hop_in(c):
         for what in range(2):
             hop_copy(c, what).wait_recv()
-        join_hop(c)
+
+    def hop_out(c):
         for what in range(2):
             go(fin_copy, c, 0, what)
 
-    def last(c):
+    def last_in(c):
         for what in range(2):
             for kind in range(2):
                 fin_copy(c, kind, what).wait_recv()
-        join_last(c)
+
+    def last_out(c):
+        @pl.when(c >= SENDS)
+        def _():
+            out_copy(c - SENDS).wait()
+
+        out_copy(c).start()
+
+    joins = ((13, last_in, join_last, last_out), (10, hop_in, join_hop, hop_out), (7, cores_in, join_cores, cores_out))
+    lag = 4
 
     def step(t, carry):
+        c = t - lag
+        busy = jnp.logical_and(c >= 0, c < chunks)
+
+        @pl.when(busy)
+        def _():
+            for late, ready, _, _ in joins:
+                stage(t, late, ready)
+            q_copy(c, 3).wait_recv()
+            for b in range(per):
+                kv_copy(c, b).wait()
+            for late, _, join, _ in joins:
+                old = t - late
+                join(jnp.where(old >= 0, old, chunks))
+            attend(c)
+            go(part_twin, c)
+            for late, _, _, pass_on in joins:
+                stage(t, late, pass_on)
+
+            @pl.when(c + KV_SLOTS < chunks)
+            def _():
+                for b in range(per):
+                    kv_copy(c + KV_SLOTS, b).start()
+
+        @pl.when(jnp.logical_not(busy))
+        def _():
+            for late, ready, join, pass_on in joins[::-1]:
+                def all_of(c, ready=ready, join=join, pass_on=pass_on):
+                    ready(c)
+                    join(c)
+                    pass_on(c)
+
+                stage(t, late, all_of)
+
         stage(t, -AHEAD, send_own)
         stage(t, 0, spread)
-        stage(t, 1, to_twin)
-        stage(t, 4, cores)
-        stage(t, 6, hop)
-        stage(t, 8, last)
-        stage(t, 2, work)
+        stage(t, 2, to_twin)
         return carry
 
-    lax.fori_loop(0, chunks + 8, step, 0)
+    lax.fori_loop(0, chunks + joins[0][0], step, 0)
     for c in range(max(chunks - SENDS, 0), chunks):
         c = jnp.int32(c)
         for kind in range(4):
             q_copy(c, kind).wait_send()
-        for what in range(2):
-            part_twin(c, what).wait_send()
+        part_twin(c).wait_send()
+        for what in range(2):
             hop_copy(c, what).wait_send()
             for kind in range(2):
                 fin_copy(c, kind, what).wait_send()
+        out_copy(c).wait()
 
 
 def solution(mesh):
@@ -280,31 +315,30 @@
             pltpu.VMEM((chunks, group, CHUNK, rows, width), bf),
             pltpu.VMEM((KV_SLOTS, CHUNK, keys, width), bf),
             pltpu.VMEM((rows, keys), jnp.int32),
-            pltpu.VMEM((KEPT, CHUNK, side, LATENT), f32),
-            pltpu.VMEM((KEPT, CHUNK, side, LANES), f32),
-            pltpu.VMEM((chunks, CHUNK, side, LATENT), bf),
-            pltpu.VMEM((chunks, CHUNK, side, LANES), f32),
-            pltpu.VMEM((chunks, CHUNK, side, LATENT), bf),
-            pltpu.VMEM((chunks, CHUNK, side, LANES), f32),
-            pltpu.VMEM((chunks, chips, block, LATENT), bf),
-            pltpu.VMEM((chunks, chips * block // LANES, 1, LANES), f32),
-            pltpu.VMEM((chunks, block, LATENT), bf),
-            pltpu.VMEM((chunks, 1, LANES), f32),
-            pltpu.VMEM((chunks, block, LATENT), bf),
-            pltpu.VMEM((chunks, 1, LANES), f32),
-            pltpu.VMEM((chunks, 2, block, LATENT), bf),
-            pltpu.VMEM((chunks, 2, 1, LANES), f32),
+            pltpu.VMEM((KEPT, CHUNK, side, LATENT + LANES), f32),
+            pltpu.VMEM((chunks, CHUNK, side, LATENT + LANES), f32),
+            pltpu.VMEM((chunks + 1, CHUNK, side, LATENT + LANES), f32),
+            pltpu.VMEM((chunks + 1, chips, block, LATENT), bf),
+            pltpu.VMEM((chunks + 1, chips * block // LANES, 1, LANES), f32),
+            pltpu.VMEM((chunks + 1, block, LATENT), bf),
+            pltpu.VMEM((chunks + 1, 1, LANES), f32),
+            pltpu.VMEM((chunks + 1, block, LATENT), bf),
+            pltpu.VMEM((chunks + 1, 1, LANES), f32),
+            pltpu.VMEM((chunks + 1, 2, block, LATENT), bf),
+            pltpu.VMEM((chunks + 1, 2, 1, LANES), f32),
+            pltpu.VMEM((chunks + 1, CHUNK, rows, LATENT), bf),
             pltpu.SemaphoreType.DMA,
             pltpu.SemaphoreType.DMA((KV_SLOTS, CHUNK)),
+            pltpu.SemaphoreType.DMA((SENDS,)),
         ]
-        for shape in ((4,), (2,), (2,), (2, 2)):
+        for shape in ((4,), (), (2,), (2, 2)):
             scratch += [pltpu.SemaphoreType.DMA((SENDS, *shape)), pltpu.SemaphoreType.DMA((chunks, *shape))]
         flops = 2 * batch * group * rows * keys * (width + LATENT)
         o = pl.pallas_call(
             functools.partial(kernel, group, rounds // 2 - 1),
-            out_shape=jax.ShapeDtypeStruct((batch, rows, LATENT), bf),
+            out_shape=jax.ShapeDtypeStruct((chunks, CHUNK, rows, LATENT), bf),
             in_specs=[pl.BlockSpec(memory_space=pltpu.SMEM), pl.BlockSpec(memory_space=pl.ANY), pl.BlockSpec(memory_space=pl.ANY)],
-            out_specs=pl.BlockSpec(memory_space=pltpu.VMEM),
+            out_specs=pl.BlockSpec(memory_space=pl.ANY),
             scratch_shapes=scratch,
             compiler_params=pltpu.CompilerParams(collective_id=0, has_side_effects=True, vmem_limit_bytes=62 * 2**20),
             cost_estimate=pl.CostEstimate(flops=flops, bytes_accessed=kv_blk.size * 2, transcendentals=batch * group * rows * keys),

time: 63.1 us -> 59.8 us (0.948); the launches traced: 62.9 us -> 58.9 us
  Pallas kernels: 61.1 us -> 57 us
    pallas_call x1, Pallas kernels: 61.1 us -> 57 us  [local_step(): pl.pallas_call(functools.partial(kernel, group, rounds // 2 - 1), out_sha...]
where the time goes in v5:
time: 59.8 us; the launch traced here: 58.9 us
  Pallas kernels  57 us (95%)
  local copies, waits for them, and re-layouts  1.87 us (3%)
    pallas_call x1, Pallas kernels, local_step(): pl.pallas_call(functools.partial(kernel, group, rounds // 2 - 1), out_sha...  57 us
    unnamed x1, local copies, waits for them, and re-layouts  1.87 us

profile of v5, /device:TPU:81, one launch (start us, length us, event | category | flops | bytes accessed | tf_op | source)
XLA Modules:
  0.0 58.9 jit_solution(914652336531526159)
XLA Ops:
  0.0 57.0 %shard_map.37 = bf16[16,2,16,512]{3,2,1,0:T(8,128)(2,1)} custom-call(s32[32]{0:T(128)} %len_ref.1, bf16[16,2,16,576]{3,2,1,0:T(8,128)(2,1)} %bitcast.5, bf16[32,1024,576]{2,1,0:T(8,128)(2,1)} %bitcast.3), custom_call_target="tpu_custom_call" | custom-call | flops 9126805504 | bytes 37748736 | tf_op jit(solution)/shard_map/pallas_call | solution.py:337
  57.0 1.9 %copy.5 = bf16[32,2,8,512]{3,2,1,0:T(8,128)(2,1)} copy(bf16[32,2,8,512]{3,2,1,0:T(8,128)(2,1)} %bitcast.4) | data formatting | bytes 1048576

commit v6 on v5

--- a/solution.py
+++ b/solution.py
@@ -13,11 +13,12 @@
 NOPE = 128
 PAGE = 64
 CORES = 2
-CHUNK = 2
-KV_SLOTS = 8
+CHUNK = 4
+KV_SLOTS = 4
 AHEAD = 2
-KEPT = 4
+KEPT = 3
 SENDS = 4
+STRAIGHT = 1
 LANES = 128
 
 
@@ -35,18 +36,20 @@
     return o_a * wide(e_a * inv, n) + o_b * wide(e_b * inv, n), top + jnp.log(total)
 
 
-def kernel(group, min_rounds, len_ref, q_hbm, kv_hbm, out_hbm, q_all, kv_buf, rank, own, sib, got, chip_o, chip_l, hop_o, hop_l, mid_o, mid_l, fin_o, fin_l,
-           out_buf, load_sem, kv_sem, out_sem, q_send, q_recv, s_send, s_recv, h_send, h_recv, f_send, f_recv):
+def kernel(group, min_rounds, len_hbm, q_hbm, kv_hbm, out_hbm, q_all, kv_buf, rank, own, sib, got, chip_o, chip_l, hop_o, hop_l, mid_o, mid_l, fin_o, fin_l,
+           out_buf, len_ref, load_sem, len_sem, kv_sem, out_sem, q_send, q_recv, s_send, s_recv, h_send, h_recv, f_send, f_recv):
     chunks, _, per, rows, width = q_all.shape
     keys = kv_buf.shape[2]
     chips = group // CORES
     side = chips * rows
     block = per * rows
+    relayed = chunks - STRAIGHT
     lot = LANES // block
     me = lax.axis_index('dcp')
     chip, core = me // CORES, me % CORES
     right = lax.rem(chip + 1, chips) * CORES + core
     left = lax.rem(chip + chips - 1, chips) * CORES + core
+    far = lax.rem(chip + 2, chips) * CORES + core
     twin = chip * CORES + (CORES - 1 - core)
     scale = (NOPE + ROPE) ** -0.5
 
@@ -77,7 +80,7 @@
     def hop_copy(c, what):
         src = (chip_o.at[c, 3], chip_l.at[c, 3 // lot])[what]
         dst = (hop_o.at[c], hop_l.at[c])[what]
-        return remote(src, dst, h_send.at[lax.rem(c, SENDS), what], h_recv.at[c, what], toward(way(c)))
+        return remote(src, dst, h_send.at[lax.rem(c, SENDS), what], h_recv.at[c, what], jnp.where(c >= relayed, far, toward(way(c))))
 
     def fin_copy(c, kind, what):
         if kind == 0:
@@ -88,6 +91,12 @@
         dst = (fin_o.at[c, kind], fin_l.at[c, kind])[what]
         return remote(src, dst, f_send.at[lax.rem(c, SENDS), kind, what], f_recv.at[c, kind, what], to)
 
+    def fin_straight(c, what):
+        slot = 2 - way(c)
+        src = (chip_o.at[c, slot], chip_l.at[c, slot // lot])[what]
+        dst = (fin_o.at[c, 0], fin_l.at[c, 0])[what]
+        return remote(src, dst, f_send.at[lax.rem(c, SENDS), 0, what], f_recv.at[c, 0, what], toward(way(c)))
+
     def out_copy(c):
         return pltpu.make_async_copy(out_buf.at[c], out_hbm.at[c], out_sem.at[lax.rem(c, SENDS)])
 
@@ -108,8 +117,10 @@
 
     load = pltpu.make_async_copy(q_hbm, q_all.at[:, 0], load_sem)
     load.start()
+    lengths = pltpu.make_async_copy(len_hbm, len_ref, len_sem)
+    lengths.start()
     barrier = pltpu.get_barrier_semaphore()
-    for peer in (left, right, twin):
+    for peer in (left, right, far, twin):
         pl.semaphore_signal(barrier, inc=1, device_id={'dcp': peer}, device_id_type=pl.DeviceIdType.MESH)
 
     r_id = lax.broadcasted_iota(jnp.int32, (rows, keys), 0)
@@ -118,7 +129,7 @@
     rank[...] = (k_id // PAGE * group + me) * PAGE + k_id % PAGE - r_id // (rows // tokens)
 
     load.wait()
-    pl.semaphore_wait(barrier, 3)
+    pl.semaphore_wait(barrier, 4)
     for c in range(min(AHEAD, chunks)):
         send_own(jnp.int32(c))
     for c in range(min(KV_SLOTS, chunks)):
@@ -188,9 +199,7 @@
         mid_o[c] = o.astype(jnp.bfloat16)
         mid_l[c] = jnp.sum(jnp.where(lane_b == row_b, lse, 0.0), axis=0, keepdims=True)
 
-    def join_last(c):
-        parts = [(chip_o[c, 0], column(chip_l[c, 0], jnp.int32(0))), (fin_o[c, 0], column(fin_l[c, 0], jnp.int32(0))),
-                 (fin_o[c, 1], column(fin_l[c, 1], 1 + way(c)))]
+    def finish(c, parts):
         top = functools.reduce(jnp.maximum, [l for _, l in parts])
         weights = [jnp.exp(l - top) for _, l in parts]
         inv = 1.0 / functools.reduce(jnp.add, weights)
@@ -199,10 +208,18 @@
         for b in range(per):
             out_buf[c, b] = o[b * rows:(b + 1) * rows]
 
-    def stage(t, lag, fn):
+    def join_last(c):
+        finish(c, [(chip_o[c, 0], column(chip_l[c, 0], jnp.int32(0))), (fin_o[c, 0], column(fin_l[c, 0], jnp.int32(0))),
+                   (fin_o[c, 1], column(fin_l[c, 1], 1 + way(c)))])
+
+    def join_straight(c):
+        finish(c, [(chip_o[c, 0], column(chip_l[c, 0], jnp.int32(0))), (fin_o[c, 0], column(fin_l[c, 0], 2 - way(c))),
+                   (fin_o[c, 1], column(fin_l[c, 1], 1 + way(c))), (hop_o[c], column(hop_l[c], jnp.int32(3)))])
+
+    def stage(t, lag, fn, start=0, stop=chunks):
         c = t - lag
 
-        @pl.when(jnp.logical_and(c >= 0, c < chunks))
+        @pl.when(jnp.logical_and(c >= start, c < stop))
         def _():
             fn(c)
 
@@ -243,10 +260,13 @@
 
         out_copy(c).start()
 
-    joins = ((13, last_in, join_last, last_out), (10, hop_in, join_hop, hop_out), (7, cores_in, join_cores, cores_out))
-    lag = 4
+    joins = ((11, last_in, join_last, last_out), (8, hop_in, join_hop, hop_out), (5, cores_in, join_cores, cores_out))
+    lag = 3
 
     def step(t, carry):
+        stage(t, -AHEAD, send_own)
+        stage(t, 0, spread)
+        stage(t, 2, to_twin)
         c = t - lag
         busy = jnp.logical_and(c >= 0, c < chunks)
 
@@ -272,19 +292,41 @@
 
         @pl.when(jnp.logical_not(busy))
         def _():
-            for late, ready, join, pass_on in joins[::-1]:
-                def all_of(c, ready=ready, join=join, pass_on=pass_on):
-                    ready(c)
-                    join(c)
-                    pass_on(c)
-
-                stage(t, late, all_of)
-
-        stage(t, -AHEAD, send_own)
-        stage(t, 0, spread)
-        stage(t, 2, to_twin)
+            def cores(c):
+                cores_in(c)
+                join_cores(c)
+                cores_out(c)
+
+            def cores_straight(c):
+                cores(c)
+                for what in range(2):
+                    go(fin_straight, c, what)
+
+            def hop(c):
+                hop_in(c)
+                join_hop(c)
+                hop_out(c)
+
+            def last(c):
+                last_in(c)
+                join_last(c)
+                last_out(c)
+
+            def last_straight(c):
+                last_in(c)
+                hop_in(c)
+                join_straight(c)
+                last_out(c)
+
+            stage(t, joins[2][0], cores, stop=relayed)
+            stage(t, joins[2][0], cores_straight, start=relayed)
+            stage(t, joins[1][0], hop, stop=relayed)
+            stage(t, joins[0][0], last, stop=relayed)
+            stage(t, joins[0][0], last_straight, start=relayed)
+
         return carry
 
+    lengths.wait()
     lax.fori_loop(0, chunks + joins[0][0], step, 0)
     for c in range(max(chunks - SENDS, 0), chunks):
         c = jnp.int32(c)
@@ -327,6 +369,8 @@
             pltpu.VMEM((chunks + 1, 2, block, LATENT), bf),
             pltpu.VMEM((chunks + 1, 2, 1, LANES), f32),
             pltpu.VMEM((chunks + 1, CHUNK, rows, LATENT), bf),
+            pltpu.SMEM((batch,), jnp.int32),
+            pltpu.SemaphoreType.DMA,
             pltpu.SemaphoreType.DMA,
             pltpu.SemaphoreType.DMA((KV_SLOTS, CHUNK)),
             pltpu.SemaphoreType.DMA((SENDS,)),
@@ -337,7 +381,7 @@
         o = pl.pallas_call(
             functools.partial(kernel, group, rounds // 2 - 1),
             out_shape=jax.ShapeDtypeStruct((chunks, CHUNK, rows, LATENT), bf),
-            in_specs=[pl.BlockSpec(memory_space=pltpu.SMEM), pl.BlockSpec(memory_space=pl.ANY), pl.BlockSpec(memory_space=pl.ANY)],
+            in_specs=[pl.BlockSpec(memory_space=pl.ANY), pl.BlockSpec(memory_space=pl.ANY), pl.BlockSpec(memory_space=pl.ANY)],
             out_specs=pl.BlockSpec(memory_space=pl.ANY),
             scratch_shapes=scratch,
             compiler_params=pltpu.CompilerParams(collective_id=0, has_side_effects=True, vmem_limit_bytes=62 * 2**20),

time: 59.8 us -> 55.1 us (0.921)
  Pallas kernels: 57 us -> 52.8 us
    pallas_call x1, Pallas kernels: 57 us -> 52.8 us  [local_step(): pl.pallas_call(functools.partial(kernel, group, rounds // 2 - 1), out_sha...]
where the time goes in v6:
time: 55.1 us; the launch traced here: 54.7 us
  Pallas kernels  52.8 us (96%)
  local copies, waits for them, and re-layouts  1.87 us (3%)
    pallas_call x1, Pallas kernels, local_step(): pl.pallas_call(functools.partial(kernel, group, rounds // 2 - 1), out_sha...  52.8 us
    unnamed x1, local copies, waits for them, and re-layouts  1.87 us

profile of v6, /device:TPU:81, one launch (start us, length us, event | category | flops | bytes accessed | tf_op | source)
XLA Modules:
  0.0 54.7 jit_solution(2610371167240708034)
XLA Ops:
  0.0 52.8 %shard_map.37 = bf16[8,4,16,512]{3,2,1,0:T(8,128)(2,1)} custom-call(s32[32]{0:T(128)} %len_hbm.1, bf16[8,4,16,576]{3,2,1,0:T(8,128)(2,1)} %bitcast.5, bf16[32,1024,576]{2,1,0:T(8,128)(2,1)} %bitcast.3), custom_call_target="tpu_custom_call" | custom-call | flops 9126805504 | bytes 37748736 | tf_op jit(solution)/shard_map/pallas_call | solution.py:381
  52.8 1.9 %copy.5 = bf16[32,2,8,512]{3,2,1,0:T(8,128)(2,1)} copy(bf16[32,2,8,512]{3,2,1,0:T(8,128)(2,1)} %bitcast.4) | data formatting | bytes 1048576
